TPU v7x, 32 devices: a whole 2x2x4 slice. The times are simulated.
32 devices in a mesh: left: 8 (over z, x), right: 4 (over y, core).
Axes of the slice: x: 2, y: 2, z: 4, core: 2. Of those that a mesh axis runs over, the one named last changes fastest.
Arguments:
- density: float32 [128, 128, 2048], P(None, 'left', 'right'), may hold values from -6 to 6
- symbol_x: float32 [128], replicated, may hold values from 0.3 to 3
- symbol_y: float32 [128], replicated, may hold values from 0.3 to 3
- symbol_z: float32 [2048], replicated, may hold values from 0.3 to 3
Outputs:
- spectrum: float32 [128, 128, 2048], P('left', 'right')
All inputs are finite; a program needn't handle non-finite values.
Results may differ from a plain program's by a relative error of at most 0.00007.
Values sent between devices are 32-bit elements; how exact they have to be, the bound alone decides.
A program may use at most 192 MiB of HBM per device.

v0:
```python
import jax
import jax.numpy as jnp
from jax import lax
from jax.sharding import PartitionSpec as P


def mode_table(count):
    rank = jnp.arange(count)
    angle = 2.0 * jnp.pi / count * (rank[:, None] * rank[None, :] % count).astype(jnp.float32)
    return (jnp.cos(angle) + jnp.sin(angle)) * count ** (-0.5)


def transform_dim(values, dim):
    moved = jnp.tensordot(
        values, mode_table(values.shape[dim]), axes=([dim], [0]), precision=lax.Precision.HIGHEST
    )
    return jnp.moveaxis(moved, -1, dim)


def per_device(density, symbol_x, symbol_y, symbol_z):
    part_values = density
    part_values = transform_dim(part_values, 0)
    part_values = lax.all_to_all(part_values, "left", split_axis=0, concat_axis=1, tiled=True)
    part_values = transform_dim(part_values, 1)
    block_values = part_values
    block_values = lax.all_to_all(block_values, "right", split_axis=1, concat_axis=2, tiled=True)
    block_values = transform_dim(block_values, 2)
    share_x = block_values.shape[0]
    part_x = lax.dynamic_slice_in_dim(symbol_x, lax.axis_index("left") * share_x, share_x)
    share_y = block_values.shape[1]
    part_y = lax.dynamic_slice_in_dim(symbol_y, lax.axis_index("right") * share_y, share_y)
    symbol = part_x[:, None, None] + part_y[None, :, None] + symbol_z[None, None, :]
    block_values = block_values * lax.rsqrt(symbol)
    return block_values


def solution(mesh):
    return jax.shard_map(
        per_device,
        mesh=mesh,
        in_specs=(P(None, "left", "right"), P(), P(), P()),
        out_specs=P("left", "right", None),
        check_vma=False,
    )
```

profile of v0, /device:TPU:0, one launch (start us, length us, event | category | flops | bytes accessed | tf_op | source)
XLA Modules:
  0.0 245.7 jit_solution(8625823502980636644)
XLA Ops:
  0.0 9.0 %fusion.19 = f32[128,16,512]{2,0,1:T(8,128)S(1)} fusion(f32[128,16,512]{2,1,0:T(8,128)} %param.4), kind=kOutput, calls=%fused_computation.20 | convolution fusion | flops 1610874880 | bytes 8388608 | tf_op jit(solution)/shard_map/dot_general | solution.py:14
  9.0 2.4 copy.24
  11.5 100.3 %all_to_all.36 = f32[128,16,512]{2,1,0:T(8,128)S(1)} all-to-all(f32[128,16,512]{2,1,0:T(8,128)S(1)} %copy.24), channel_id=1, replica_groups=mesh['left'=8,'right'=4] {'left'}, dimensions={0} | all-to-all | bytes 8388608 | tf_op jit(solution)/shard_map/all_to_all | solution.py:23
  111.7 0.8 copy.25
  112.6 8.6 %convolution_bitcast_fusion = f32[16,128,512]{1,2,0:T(8,128)} fusion(f32[16,128,512]{2,1,0:T(8,128)S(1)} %bitcast.28), kind=kOutput, calls=%fused_computation.23 | convolution fusion | flops 1610874880 | bytes 8388608 | tf_op jit(solution)/shard_map/dot_general | solution.py:14
  121.2 5.5 %copy.27 = f32[16,128,512]{2,0,1:T(8,128)} copy(f32[16,128,512]{1,2,0:T(8,128)} %convolution_bitcast_fusion) | data formatting | bytes 8388608 | tf_op jit(solution)/shard_map/transpose | solution.py:17
  126.7 0.0 copy-start.1
  126.7 0.0 copy-start.2
  126.7 5.1 %all-to-all-start.1 = ((f32[16,128,512]{2,0,1:T(8,128)}), f32[16,128,512]{2,0,1:T(8,128)}, u32[]{:S(2)}, u32[]{:S(2)}) async-start(f32[16,128,512]{2,0,1:T(8,128)} %copy.27), calls=%async_computation.1 | async-start | bytes 8388608 | tf_op jit(solution)/shard_map/all_to_all | solution.py:26
  131.8 0.0 copy-done.1
  131.9 0.1 dynamic_slice.7
  131.9 0.0 copy-done.2
  131.9 0.1 dynamic_slice.6
  132.0 0.1 broadcast_add_fusion
  132.1 67.7 %fusion.51 = f32[2048,2048,1]{1,0,2:T(8,128)} fusion(), kind=kLoop, calls=%fused_computation.7.clone.clone.clone.1 | loop fusion | flops 67108864 | bytes 16777216 | tf_op jit(solution)/shard_map/dot_general | solution.py:14
  199.8 0.0 all-to-all-done.1
  199.8 6.9 %copy.29 = f32[16,32,4,512]{3,2,1,0:T(4,128)} copy(f32[16,32,4,512]{3,0,1,2:T(8,128)} %bitcast.8) | data formatting | bytes 8388608 | tf_op jit(solution)/shard_map/all_to_all | solution.py:26
  206.7 0.0 copy-start
  206.7 6.1 %all_to_all.33 = f32[16,32,2048]{2,1,0:T(8,128)} reshape(f32[16,32,4,512]{3,2,1,0:T(4,128)} %copy.29) | data formatting | bytes 8388608 | tf_op jit(solution)/shard_map/all_to_all | solution.py:26
  212.7 0.0 copy-done
  212.8 33.0 %rsqrt_multiply_fusion = f32[16,32,2048]{2,1,0:T(8,128)} fusion(f32[16,32,2048]{2,1,0:T(8,128)} %all_to_all.33, f32[2048]{0:T(1024)S(1)} %copy-done, f32[16,32]{1,0:T(8,128)S(1)} %broadcast_add_fusion, f32[2048,2048,1]{1,0,2:T(8,128)} %fusion.51), kind=kOutput, calls=%fused_computation.22 | convolution fusion | flops 25771900928 | bytes 25176064 | tf_op jit(solution)/shard_map/dot_general | solution.py:14
Async XLA Ops:
  126.7 5.2 %copy-start.1 = (f32[128]{0:T(128)S(1)}, f32[128]{0:T(128)}, u32[]{:S(2)}) copy-start(f32[128]{0:T(128)} %param.6) | copy-start | bytes 1540
  126.7 5.3 %copy-start.2 = (f32[128]{0:T(128)S(1)}, f32[128]{0:T(128)}, u32[]{:S(2)}) copy-start(f32[128]{0:T(128)} %param.5) | copy-start | bytes 1540
  126.7 73.1 %all-to-all-start.1 = ((f32[16,128,512]{2,0,1:T(8,128)}), f32[16,128,512]{2,0,1:T(8,128)}, u32[]{:S(2)}, u32[]{:S(2)}) async-start(f32[16,128,512]{2,0,1:T(8,128)} %copy.27), calls=%async_computation.1 | async-start | bytes 8388608 | tf_op jit(solution)/shard_map/all_to_all | solution.py:26
  206.7 6.1 %copy-start = (f32[2048]{0:T(1024)S(1)}, f32[2048]{0:T(1024)}, u32[]{:S(2)}) copy-start(f32[2048]{0:T(1024)} %param.7) | copy-start | bytes 24580
where the time goes:
time: 246 us
  blocking collectives  100 us (41%)
  other arithmetic  67.8 us (28%)
  matrix products  50.6 us (21%)
  local copies, waits for them, and re-layouts  21.9 us (9%)
  starting transfers between devices  5.15 us (2%)
    all_to_all x1, blocking collectives, per_device(): lax.all_to_all(part_values, 'left', split_axis=0, concat_axis=1, tiled=True)  100 us
    dot_general x1, other arithmetic, transform_dim(): jnp.tensordot(values, mode_table(values.shape[dim]), axes=([dim], [0]), p...  67.7 us
    dot_general x3, matrix products, transform_dim(): jnp.tensordot(values, mode_table(values.shape[dim]), axes=([dim], [0]), p...  50.6 us
    all_to_all x2, local copies, waits for them, and re-layouts, per_device(): lax.all_to_all(block_values, 'right', split_axis=1, concat_axis=2, tiled=...  13 us
    transpose x1, local copies, waits for them, and re-layouts, transform_dim(): return jnp.moveaxis(moved, -1, dim)  5.51 us
    all_to_all x1, starting transfers between devices, per_device(): lax.all_to_all(block_values, 'right', split_axis=1, concat_axis=2, tiled=...  5.15 us
  transfers between devices with their start and end apart: 1, of which 0 were waited for; matrix products, arithmetic and copies ran while one was open for 28% of the time, Pallas kernels for 0%

commit v1 on v0

--- a/solution.py
+++ b/solution.py
@@ -23,7 +23,10 @@
     part_values = lax.all_to_all(part_values, "left", split_axis=0, concat_axis=1, tiled=True)
     part_values = transform_dim(part_values, 1)
     block_values = part_values
-    block_values = lax.all_to_all(block_values, "right", split_axis=1, concat_axis=2, tiled=True)
+    n_dev = lax.axis_size("right")
+    blocks = jnp.stack(jnp.split(block_values, n_dev, axis=1), axis=0)
+    blocks = lax.all_to_all(blocks, "right", split_axis=0, concat_axis=0)
+    block_values = jnp.concatenate(blocks, axis=2)
     block_values = transform_dim(block_values, 2)
     share_x = block_values.shape[0]
     part_x = lax.dynamic_slice_in_dim(symbol_x, lax.axis_index("left") * share_x, share_x)

time: 246 us -> 227 us (0.923)
  local copies, waits for them, and re-layouts: 21.9 us -> 6.86 us
  matrix products: 50.6 us -> 43.9 us
  other arithmetic: 67.8 us -> 70.3 us
    all_to_all x2 -> x0, local copies, waits for them, and re-layouts: 13 us -> none  [per_device(): lax.all_to_all(block_values, 'right', split_axis=1, concat_axis=2, tiled=...]
    dot_general x3, matrix products: 50.6 us -> 43.9 us  [transform_dim(): jnp.tensordot(values, mode_table(values.shape[dim]), axes=([dim], [0]), p...]
    transpose x1 -> x0, local copies, waits for them, and re-layouts: 5.51 us -> none  [transform_dim(): return jnp.moveaxis(moved, -1, dim)]
    reshape x0 -> x1, local copies, waits for them, and re-layouts: none -> 2.64 us  [per_device(): block_values = jnp.concatenate(blocks, axis=2)]
    another operation x0 -> x1, other arithmetic: none -> 2.52 us  [per_device(): blocks = jnp.stack(jnp.split(block_values, n_dev, axis=1), axis=0)]
  transfers between devices with their start and end apart: 1 -> 1, of which waited for: 0 -> 0; matrix products, arithmetic and copies ran while one was open for 28% -> 30% of each run, Pallas kernels for 0% -> 0%
where the time goes in v1:
time: 227 us
  blocking collectives  100 us (44%)
  other arithmetic  70.3 us (31%)
  matrix products  43.9 us (19%)
  local copies, waits for them, and re-layouts  6.86 us (3%)
  starting transfers between devices  5.2 us (2%)
    all_to_all x1, blocking collectives, per_device(): lax.all_to_all(part_values, 'left', split_axis=0, concat_axis=1, tiled=True)  100 us
    dot_general x1, other arithmetic, transform_dim(): jnp.tensordot(values, mode_table(values.shape[dim]), axes=([dim], [0]), p...  67.7 us
    dot_general x3, matrix products, transform_dim(): jnp.tensordot(values, mode_table(values.shape[dim]), axes=([dim], [0]), p...  43.9 us
    all_to_all x1, starting transfers between devices, per_device(): blocks = lax.all_to_all(blocks, 'right', split_axis=0, concat_axis=0)  5.2 us
  transfers between devices with their start and end apart: 1, of which 0 were waited for; matrix products, arithmetic and copies ran while one was open for 30% of the time, Pallas kernels for 0%

profile of v1, /device:TPU:0, one launch (start us, length us, event | category | flops | bytes accessed | tf_op | source)
XLA Modules:
  0.0 226.6 jit_solution(9537511097673726067)
XLA Ops:
  0.0 8.4 %fusion.19 = f32[128,16,512]{2,0,1:T(8,128)S(1)} fusion(f32[128,16,512]{2,1,0:T(8,128)} %param.4), kind=kOutput, calls=%fused_computation.21 | convolution fusion | flops 1610874880 | bytes 8388608 | tf_op jit(solution)/shard_map/dot_general | solution.py:14
  8.5 2.4 %copy.11 = f32[128,16,512]{2,1,0:T(8,128)S(1)} copy(f32[128,16,512]{2,0,1:T(8,128)S(1)} %fusion.19) | data formatting | bytes 8388608 | tf_op jit(solution)/shard_map/dot_general | solution.py:14
  10.9 100.3 %all_to_all.23 = f32[128,16,512]{2,1,0:T(8,128)S(1)} all-to-all(f32[128,16,512]{2,1,0:T(8,128)S(1)} %copy.11), channel_id=1, replica_groups=mesh['left'=8,'right'=4] {'left'}, dimensions={0} | all-to-all | bytes 8388608 | tf_op jit(solution)/shard_map/all_to_all | solution.py:23
  111.2 0.8 copy.12
  112.0 4.7 %convolution_bitcast_fusion = f32[16,128,512]{2,1,0:T(8,128)S(1)} fusion(f32[16,128,512]{2,1,0:T(8,128)S(1)} %bitcast.35), kind=kOutput, calls=%fused_computation.24 | convolution fusion | flops 1610874880 | bytes 8388608 | tf_op jit(solution)/shard_map/dot_general | solution.py:14
  116.7 0.8 slice_bitcast_fusion.3
  117.5 2.5 %pad_maximum_fusion = f32[4,16,32,512]{3,2,1,0:T(8,128)} fusion(f32[1,16,32,512]{3,2,1,0:T(8,128)S(1)} %get-tuple-element.6, f32[1,16,32,512]{3,2,1,0:T(8,128)S(1)} %get-tuple-element.7, f32[1,16,32,512]{3,2,1,0:T(8,128)S(1)} %get-tuple-element.8, f32[1,16,32,512]{3,2,1,0:T(8,128)S(1)} %get-tuple-element.5), kind=kLoop, calls=%fused_computation.20 | loop fusion | flops 3145728 | bytes 8388608 | tf_op jit(solution)/shard_map/stack | solution.py:27
  120.0 0.0 copy-start.1
  120.0 0.0 copy-start.2
  120.0 5.2 %all-to-all-start.1 = ((f32[4,16,32,512]{3,2,1,0:T(8,128)}), f32[4,16,32,512]{3,2,1,0:T(8,128)}, u32[]{:S(2)}, u32[]{:S(2)}) async-start(f32[4,16,32,512]{3,2,1,0:T(8,128)} %pad_maximum_fusion), calls=%async_computation.1 | async-start | bytes 8388608 | tf_op jit(solution)/shard_map/all_to_all | solution.py:28
  125.3 0.0 copy-done.1
  125.3 0.1 dynamic_slice.7
  125.4 0.0 copy-done.2
  125.4 0.1 dynamic_slice.6
  125.4 0.1 broadcast_add_fusion
  125.5 67.7 %fusion.51 = f32[2048,2048,1]{1,0,2:T(8,128)} fusion(), kind=kLoop, calls=%fused_computation.7.clone.clone.clone.1 | loop fusion | flops 67108864 | bytes 16777216 | tf_op jit(solution)/shard_map/dot_general | solution.py:14
  193.2 0.0 all-to-all-done.1
  193.2 0.0 copy-start
  193.2 2.6 %copy.14 = f32[4,16,4,8,512]{4,3,0,2,1:T(8,128)S(1)} copy(f32[4,16,4,8,512]{4,3,2,1,0:T(8,128)} %bitcast.12) | data formatting | bytes 8388608 | tf_op jit(solution)/shard_map/reshape | solution.py:29
  195.8 0.0 copy-done
  195.8 30.7 %rsqrt_multiply_fusion = f32[16,32,2048]{2,1,0:T(8,128)} fusion(f32[16,32,2048]{2,1,0:T(8,128)S(1)} %bitcast.36, f32[2048]{0:T(1024)S(1)} %copy-done, f32[16,32]{1,0:T(8,128)S(1)} %broadcast_add_fusion, f32[2048,2048,1]{1,0,2:T(8,128)} %fusion.51), kind=kOutput, calls=%fused_computation.23 | convolution fusion | flops 25771900928 | bytes 25176064 | tf_op jit(solution)/shard_map/dot_general | solution.py:14
Async XLA Ops:
  120.0 5.2 %copy-start.1 = (f32[128]{0:T(128)S(1)}, f32[128]{0:T(128)}, u32[]{:S(2)}) copy-start(f32[128]{0:T(128)} %param.6) | copy-start | bytes 1540
  120.0 5.3 %copy-start.2 = (f32[128]{0:T(128)S(1)}, f32[128]{0:T(128)}, u32[]{:S(2)}) copy-start(f32[128]{0:T(128)} %param.5) | copy-start | bytes 1540
  120.0 73.1 %all-to-all-start.1 = ((f32[4,16,32,512]{3,2,1,0:T(8,128)}), f32[4,16,32,512]{3,2,1,0:T(8,128)}, u32[]{:S(2)}, u32[]{:S(2)}) async-start(f32[4,16,32,512]{3,2,1,0:T(8,128)} %pad_maximum_fusion), calls=%async_computation.1 | async-start | bytes 8388608 | tf_op jit(solution)/shard_map/all_to_all | solution.py:28
  193.2 2.6 %copy-start = (f32[2048]{0:T(1024)S(1)}, f32[2048]{0:T(1024)}, u32[]{:S(2)}) copy-start(f32[2048]{0:T(1024)} %param.7) | copy-start | bytes 24580
